TPU v7x, 32 devices: a whole 2x2x4 slice. The times are simulated.
32 devices in a mesh: seq: 16 (over z, x, core), head: 2 (over y).
Axes of the slice: x: 2, y: 2, z: 4, core: 2. Of those that a mesh axis runs over, the one named last changes fastest.
Arguments:
- query_rows: bfloat16 [3072, 2048], P('seq', 'head'), may hold values from -6 to 6
- key_rows: bfloat16 [3072, 2048], P('seq', 'head'), may hold values from -6 to 6
- value_rows: bfloat16 [3072, 2048], P('seq', 'head'), may hold values from -6 to 6
- grad_output: bfloat16 [3072, 2048], P('seq', 'head'), may hold values from -6 to 6
- positions: int32 [3072], P('seq'), may hold values from 0 to 3071, each once
Outputs:
- grad_query: bfloat16 [3072, 2048], P(('seq', 'head'))
- grad_keys: bfloat16 [3072, 2048], P('seq', 'head')
- grad_values: bfloat16 [3072, 2048], P('seq', 'head')
Inputs may be any that keep to these rules, and one draw needn't show every extreme that they name: `positions`: each number from 0 to 3071 appears once.
All inputs are finite; a program needn't handle non-finite values.
Results may differ from a plain program's by a relative error of at most 0.012.
Values may be sent and summed in bfloat16 or wider, within the bound.
A program may use at most 128 MiB of HBM per device.

v0:
```python
import jax
import jax.numpy as jnp
from jax import lax
from jax.sharding import PartitionSpec as P

HEAD_DIM = 128


def split_heads(matrix):
    return matrix.reshape(matrix.shape[0], matrix.shape[1] // HEAD_DIM, HEAD_DIM)


def join_heads(tensor):
    return tensor.reshape(tensor.shape[0], tensor.shape[1] * tensor.shape[2])


def stats_update(running, query_heads, grad_heads, query_pos, key_block, value_block, key_pos):
    maximum, denominator, delta_sum = running
    scaling = HEAD_DIM ** (-0.5)
    scores = (
        jnp.einsum("qhd,khd->hqk", query_heads, key_block, preferred_element_type=jnp.float32)
        * scaling
    )
    allowed = (key_pos[None, :] <= query_pos[:, None])[None]
    masked = jnp.where(allowed, scores, -1e30)
    new_max = jnp.maximum(maximum, jnp.max(masked, axis=2))
    unscaled = jnp.where(allowed, jnp.exp(masked - new_max[:, :, None]), 0.0)
    grad_probs = jnp.einsum(
        "qhd,khd->hqk", grad_heads, value_block, preferred_element_type=jnp.float32
    )
    denominator = jnp.sum(unscaled, axis=2)
    delta_sum = jnp.sum(unscaled * grad_probs, axis=2)
    return (new_max, denominator, delta_sum)


def gradient_terms(
    query_heads, grad_heads, query_pos, log_total, row_delta, key_block, value_block, key_pos
):
    scaling = HEAD_DIM ** (-0.5)
    scores = (
        jnp.einsum("qhd,khd->hqk", query_heads, key_block, preferred_element_type=jnp.float32)
        * scaling
    )
    allowed = (key_pos[None, :] <= query_pos[:, None])[None]
    masked = jnp.where(allowed, scores, -1e30)
    probabilities = jnp.where(allowed, jnp.exp(masked - log_total[:, :, None]), 0.0)
    weights = probabilities.astype(jnp.bfloat16)
    grad_value = jnp.einsum("hqk,qhd->khd", weights, grad_heads, preferred_element_type=jnp.float32)
    grad_probs = jnp.einsum(
        "qhd,khd->hqk", grad_heads, value_block, preferred_element_type=jnp.float32
    )
    grad_scores = (probabilities * (grad_probs - row_delta[:, :, None]) * scaling).astype(
        jnp.bfloat16
    )
    grad_query = jnp.einsum(
        "hqk,khd->qhd", grad_scores, key_block, preferred_element_type=jnp.float32
    )
    grad_key = jnp.einsum(
        "hqk,qhd->khd", grad_scores, query_heads, preferred_element_type=jnp.float32
    )
    return (grad_query, grad_key, grad_value)


def local(query_rows, key_rows, value_rows, grad_output, positions):
    row_count = query_rows.shape[0]
    head_count = query_rows.shape[1] // HEAD_DIM
    members = lax.axis_size("seq")
    query_heads = split_heads(query_rows)
    grad_heads = split_heads(grad_output)
    start_running = (
        jnp.full((head_count, row_count), -1e30, jnp.float32),
        jnp.zeros((head_count, row_count), jnp.float32),
        jnp.zeros((head_count, row_count), jnp.float32),
    )
    start_copies = (
        jnp.zeros((row_count * members, key_rows.shape[1]), key_rows.dtype),
        jnp.zeros((row_count * members, value_rows.shape[1]), value_rows.dtype),
        jnp.zeros((row_count * members,), jnp.int32),
    )
    start_carry = (start_running, start_copies)
    portion = (
        lax.all_gather(key_rows, "seq", axis=0, tiled=True),
        lax.all_gather(value_rows, "seq", axis=0, tiled=True),
        lax.all_gather(positions, "seq", axis=0, tiled=True),
    )
    offset = jnp.int32(0)
    stats = stats_update(
        start_carry[0],
        query_heads,
        grad_heads,
        positions,
        split_heads(portion[0]),
        split_heads(portion[1]),
        portion[2],
    )
    copies = tuple(
        (
            lax.dynamic_update_slice_in_dim(held_copy, piece, offset, 0)
            for held_copy, piece in zip(start_carry[1], portion)
        )
    )
    maximum, denominator, delta_sum = stats
    log_total = maximum + jnp.log(denominator)
    row_delta = delta_sum / denominator
    key_copy, value_copy, pos_copy = copies
    full_shape = (row_count * members, head_count, HEAD_DIM)

    def held_turn(block_index, carried):
        query_sum, key_full, value_full = carried
        begin = block_index * row_count
        key_block = split_heads(lax.dynamic_slice_in_dim(key_copy, begin, row_count, 0))
        value_block = split_heads(lax.dynamic_slice_in_dim(value_copy, begin, row_count, 0))
        pos_block = lax.dynamic_slice_in_dim(pos_copy, begin, row_count, 0)
        pieces = gradient_terms(
            query_heads,
            grad_heads,
            positions,
            log_total,
            row_delta,
            key_block,
            value_block,
            pos_block,
        )
        key_full = lax.dynamic_update_slice_in_dim(key_full, pieces[1], begin, 0)
        value_full = lax.dynamic_update_slice_in_dim(value_full, pieces[2], begin, 0)
        return (query_sum + pieces[0], key_full, value_full)

    start_held = (
        jnp.zeros((row_count, head_count, HEAD_DIM), jnp.float32),
        jnp.zeros(full_shape, jnp.float32),
        jnp.zeros(full_shape, jnp.float32),
    )
    grad_query, key_full, value_full = lax.fori_loop(0, members, held_turn, start_held)
    grad_keys, grad_values = (
        lax.psum_scatter(key_full, "seq", scatter_dimension=0, tiled=True),
        lax.psum_scatter(value_full, "seq", scatter_dimension=0, tiled=True),
    )
    regrouped = lax.all_to_all(
        join_heads(grad_query).astype(jnp.bfloat16), "head", split_axis=0, concat_axis=1, tiled=True
    )
    return (
        regrouped,
        join_heads(grad_keys).astype(jnp.bfloat16),
        join_heads(grad_values).astype(jnp.bfloat16),
    )


def solution(mesh):
    placed = (P("seq", "head"), P("seq", "head"), P("seq", "head"), P("seq", "head"), P("seq"))
    return jax.shard_map(
        local,
        mesh=mesh,
        in_specs=placed,
        out_specs=(P(("seq", "head"), None), P("seq", "head"), P("seq", "head")),
        check_vma=False,
    )
```

profile of v0, /device:TPU:0, one launch (start us, length us, event | category | flops | bytes accessed | tf_op | source)
XLA Modules:
  0.0 536.5 jit_solution(7610476858277274957)
XLA Ops:
  8.7 1.2 dynamic-slice
  11.5 65.2 %all-reduce = s32[3072]{0:T(1024)S(1)} all-reduce(s32[3072]{0:T(1024)S(1)} %dynamic-update-slice), channel_id=1, replica_groups=mesh['seq'=16,'head'=2] {'seq'}, use_global_device_ids=true, to_apply=%add | all-reduce | flops 3072 | bytes 24576
  79.1 8.7 %copy.54 = bf16[3072,1024]{0,1:T(8,128)(2,1)} copy(bf16[3072,1024]{1,0:T(8,128)(2,1)} %all-gather.3.cloned.1.call-done) | data formatting | bytes 12582912 | tf_op jit(solution)/shard_map/all_gather | solution.py:82
  87.8 13.3 %fusion.15 = (f32[8,192]{1,0:T(8,128)S(1)}, f32[8,192,3072]{2,1,0:T(8,128)}) fusion(pred[192,3072]{1,0:T(8,128)(4,1)S(1)} %broadcast_compare_fusion.1, bf16[3072,8,128]{0,2,1:T(8,128)(2,1)} %bitcast.112, bf16[192,1024]{1,0:T(8,128)(2,1)S(1)} %copy-done), kind=kOutput, calls=%fused_computation.26 | convolution fusion | flops 1222113792 | bytes 26155008 | tf_op jit(solution)/shard_map/qhd,khd->hqk/dot_general | solution.py:21
  101.1 12.6 %fusion.16 = f32[8,192]{1,0:T(8,128)S(1)} fusion(f32[8,192,3072]{2,1,0:T(8,128)} %get-tuple-element.311, f32[8,192]{1,0:T(8,128)S(1)} %broadcast_maximum_fusion, pred[192,3072]{1,0:T(8,128)(4,1)S(1)} %broadcast_compare_fusion.1), kind=kLoop, calls=%fused_computation.27 | loop fusion | flops 23591424 | bytes 19476480 | tf_op jit(solution)/shard_map/reduce_sum | solution.py:31
  113.7 23.8 %all-gather.5.cloned.1.call-done = bf16[3072,1024]{1,0:T(8,128)(2,1)} async-done(((bf16[192,1024]{1,0:T(8,128)(2,1)}), bf16[3072,1024]{1,0:T(8,128)(2,1)}) %all-gather.5.cloned.1.call-update) | async-done | bytes 6291472 | tf_op jit(solution)/shard_map/all_gather | solution.py:83
  137.5 8.7 %copy.57 = bf16[3072,1024]{0,1:T(8,128)(2,1)} copy(bf16[3072,1024]{1,0:T(8,128)(2,1)} %all-gather.5.cloned.1.call-done) | data formatting | bytes 12582912 | tf_op jit(solution)/shard_map/all_gather | solution.py:83
  146.2 12.0 %multiply_reduce_fusion = f32[8,192]{1,0:T(8,128)S(1)} fusion(f32[8,192,3072]{2,1,0:T(8,128)} %get-tuple-element.311, f32[8,192]{1,0:T(8,128)S(1)} %broadcast_maximum_fusion, pred[192,3072]{1,0:T(8,128)(4,1)S(1)} %broadcast_compare_fusion.1, bf16[3072,8,128]{0,2,1:T(8,128)(2,1)} %bitcast.113, bf16[192,1024]{1,0:T(8,128)(2,1)S(1)} %copy-done.2), kind=kOutput, calls=%fused_computation.23 | convolution fusion | flops 1236269568 | bytes 26161152 | tf_op jit(solution)/shard_map/qhd,khd->hqk/dot_general | solution.py:28
  158.2 5.6 %broadcast.61 = f32[3072,8,128]{2,0,1:T(8,128)} broadcast(f32[]{:T(128)} %constant.55.clone.1), dimensions={} | broadcast | bytes 12582916 | tf_op jit(solution)/shard_map/broadcast.3
  163.8 5.5 %broadcast.61.clone = f32[3072,8,128]{2,0,1:T(8,128)} broadcast(f32[]{:T(128)} %constant.55.clone.1), dimensions={} | broadcast | bytes 12582916 | tf_op jit(solution)/shard_map/broadcast.3
  169.3 87.0 %while.18 = (s32[]{:T(128)}, f32[192,8,128]{2,0,1:T(8,128)S(1)}, f32[3072,8,128]{2,0,1:T(8,128)}, f32[3072,8,128]{2,0,1:T(8,128)}, bf16[3072,1024]{1,0:T(8,128)(...) while((s32[]{:T(128)}, f32[192,8,128]{2,0,1:T(8,128)S(1)}, ...), condition=%wide.region_4.5_spmd.clone, body=%wide.region_3.4_spmd.clone.sunk | while | flops 380571648 | bytes 12868829 | solution.py:133
  171.6 1.3 fusion.59
  172.9 1.3 fusion.60
  177.1 1.3 fusion.59
  178.4 1.3 fusion.60
  182.6 1.3 fusion.59
  183.9 1.3 fusion.60
  188.0 1.3 fusion.59
  189.3 1.2 fusion.60
  193.5 1.3 fusion.59
  194.7 1.2 fusion.60
  198.9 1.2 fusion.59
  200.1 1.2 fusion.60
  204.3 1.3 fusion.59
  205.5 1.3 fusion.60
  209.7 1.3 fusion.59
  211.0 1.2 fusion.60
  215.1 1.3 fusion.59
  216.4 1.3 fusion.60
  220.6 1.2 fusion.59
  221.8 1.3 fusion.60
  226.0 1.2 fusion.59
  227.3 1.2 fusion.60
  231.4 1.3 fusion.59
  232.7 1.3 fusion.60
  236.8 1.3 fusion.59
  238.2 1.3 fusion.60
  242.3 1.3 fusion.59
  243.6 1.3 fusion.60
  247.8 1.3 fusion.59
  249.1 1.3 fusion.60
  253.2 1.2 fusion.59
  254.5 1.3 fusion.60
  257.4 9.7 %all_to_all.16 = bf16[2,96,1024]{2,1,0:T(8,128)(2,1)S(1)} all-to-all(bf16[2,96,1024]{2,1,0:T(8,128)(2,1)S(1)} %convert_element_type.34), channel_id=1, replica_groups=mesh['seq'=16,'head'=2] {'head'}, dimensions={0} | all-to-all | bytes 786432 | tf_op jit(solution)/shard_map/all_to_all | solution.py:138
  267.9 122.2 %reduce-scatter.5.cloned.1.call-done = f32[192,8,128]{2,0,1:T(8,128)} async-done(((f32[3072,8,128]{2,0,1:T(8,128)}), f32[192,8,128]{2,0,1:T(8,128)}) %reduce-scatter.5.cloned.1.call-update) | async-done | bytes 786448 | tf_op jit(solution)/shard_map/reduce_scatter | solution.py:136
  390.0 1.9 copy_bitcast_fusion
  392.0 136.1 %reduce-scatter.3.cloned.1.call-done = f32[192,8,128]{2,0,1:T(8,128)} async-done(((f32[3072,8,128]{2,0,1:T(8,128)}), f32[192,8,128]{2,0,1:T(8,128)}) %reduce-scatter.3.cloned.1.call-update) | async-done | bytes 786448 | tf_op jit(solution)/shard_map/reduce_scatter | solution.py:135
  528.0 1.9 copy_bitcast_fusion.1
  (124 shorter events, 52.2 us)
Async XLA Ops:
  7.2 69.6 %copy-start = (bf16[192,1024]{1,0:T(8,128)(2,1)S(1)}, bf16[192,1024]{1,0:T(8,128)(2,1)}, u32[]{:S(2)}) copy-start(bf16[192,1024]{1,0:T(8,128)(2,1)} %param.7) | copy-start | bytes 1179652
  7.2 71.9 %all-gather.3.cloned.1.call-start = ((), (), s32[]{:S(2)}) async-start(), calls=%async_computation.3 | async-start | bytes 6684672 | tf_op jit(solution)/shard_map/all_gather | solution.py:82
  7.9 129.6 %all-gather.5.cloned.1.call-start = ((), (), s32[]{:S(2)}) async-start(), calls=%async_computation.4 | async-start | bytes 6684672 | tf_op jit(solution)/shard_map/all_gather | solution.py:83
  8.7 381.4 %reduce-scatter.5.cloned.1.call-start = ((), (), s32[]{:S(2)}) async-start(), calls=%async_computation.6 | async-start | bytes 13369344 | tf_op jit(solution)/shard_map/reduce_scatter | solution.py:136
  101.1 45.1 %copy-start.2 = (bf16[192,1024]{1,0:T(8,128)(2,1)S(1)}, bf16[192,1024]{1,0:T(8,128)(2,1)}, u32[]{:S(2)}) copy-start(bf16[192,1024]{1,0:T(8,128)(2,1)} %param.10) | copy-start | bytes 1179652
  158.2 11.1 %copy-start.3 = (s32[192]{0:T(256)S(1)}, s32[192]{0:T(256)}, u32[]{:S(2)}) copy-start(s32[192]{0:T(256)} %param.11) | copy-start | bytes 2308
  256.3 273.7 %copy-start.1 = (bf16[192,1024]{1,0:T(8,128)(2,1)S(1)}, bf16[192,1024]{1,0:T(8,128)(2,1)}, u32[]{:S(2)}) copy-start(bf16[192,1024]{1,0:T(8,128)(2,1)} %param.7) | copy-start | bytes 1179652
  256.3 271.7 %reduce-scatter.3.cloned.1.call-start = ((), (), s32[]{:S(2)}) async-start(), calls=%async_computation.5 | async-start | bytes 13369344 | tf_op jit(solution)/shard_map/reduce_scatter | solution.py:135
Sparse Core Ops, SparseCore 0:
  10.3 64.7 all-gather.2
  77.3 60.1 all-gather.4
  256.5 133.5 reduce-scatter.4
  393.9 134.0 reduce-scatter.2
where the time goes:
time: 538 us; the launch traced here: 537 us
  waiting for transfers between devices  284 us (53%)
  matrix products  89.8 us (17%)
  blocking collectives  74.9 us (14%)
  local copies, waits for them, and re-layouts  53.1 us (10%)
  other arithmetic  19.1 us (4%)
  between operations  14.5 us (3%)
    reduce_scatter x1, waiting for transfers between devices, local(): lax.psum_scatter(key_full, 'seq', scatter_dimension=0, tiled=True)  136 us
    reduce_scatter x1, waiting for transfers between devices, local(): lax.psum_scatter(value_full, 'seq', scatter_dimension=0, tiled=True)  122 us
    unnamed x1, blocking collectives  65.2 us
    all_gather x1, waiting for transfers between devices, local(): lax.all_gather(value_rows, 'seq', axis=0, tiled=True)  23.8 us
    dot_general x16, matrix products, gradient_terms(): jnp.einsum('hqk,qhd->khd', grad_scores, query_heads, preferred_element_ty...  20.3 us
    dot_general x16, matrix products, gradient_terms(): jnp.einsum('hqk,qhd->khd', weights, grad_heads, preferred_element_type=jn...  20.1 us
    while x16, local copies, waits for them, and re-layouts  18.7 us
    dot_general x1, matrix products, stats_update(): jnp.einsum('qhd,khd->hqk', query_heads, key_block, preferred_element_type...  13.3 us
  transfers between devices with their start and end apart: 4, of which 3 were waited for; matrix products, arithmetic and copies ran while one was open for 8% of the time, Pallas kernels for 0%

commit v1 on v0

v1 whole, which is shorter than its diff:
```python
import functools

import jax
import jax.numpy as jnp
from jax import lax
from jax.experimental import pallas as pl
from jax.experimental.pallas import tpu as pltpu
from jax.sharding import PartitionSpec as P

HEAD_DIM = 128
MESH = pl.DeviceIdType.MESH
NT = (((1,), (1,)), ((), ()))
TN = (((0,), (0,)), ((), ()))


def kernel(
    members, heads, groups, rows, width,
    pos_ref, q_hbm, k_hbm, v_hbm, g_hbm,
    dq_out, dk_out, dv_out,
    q_buf, g_buf, k_buf, v_buf, pos_buf, key_pos, query_pos,
    z_buf, p_buf, dk_acc, dv_acc, dq_acc, kv_stage, kv_mates, kv_final, kv_back, dq_stage, dq_back,
    local_sem, in_send, in_recv, pos_send, pos_recv, mate_send, mate_recv,
    part_send, part_recv, back_send, back_recv, dq_send, dq_recv,
):
    ratio = members // heads
    me = lax.axis_index("seq")
    group = lax.axis_index("head")
    mine = me // ratio
    lane = lax.rem(me, ratio)
    scaling = HEAD_DIM ** (-0.5)

    barrier = pltpu.get_barrier_semaphore()
    for d in range(1, members):
        pl.semaphore_signal(
            barrier, inc=1,
            device_id={"seq": lax.rem(me + d, members), "head": group}, device_id_type=MESH,
        )
    for e in range(1, groups):
        for j in range(heads):
            pl.semaphore_signal(
                barrier, inc=1,
                device_id={
                    "seq": lax.rem(mine + j, heads) * ratio + lane,
                    "head": lax.rem(group + e, groups),
                },
                device_id_type=MESH,
            )
    pl.semaphore_wait(barrier, members - 1 + (groups - 1) * heads)

    def columns(index):
        return pl.ds(pl.multiple_of(index * HEAD_DIM, HEAD_DIM), HEAD_DIM)

    my_slot = lane * heads + mine
    pairs = (
        (k_hbm, k_buf, my_slot), (v_hbm, v_buf, my_slot), (q_hbm, q_buf, mine), (g_hbm, g_buf, mine)
    )
    pos_copies = []
    for d in range(1, members):
        copy = pltpu.make_async_remote_copy(
            src_ref=pos_ref, dst_ref=pos_buf.at[my_slot],
            send_sem=pos_send.at[d], recv_sem=pos_recv.at[d],
            device_id={"seq": lax.rem(me + d, members), "head": group}, device_id_type=MESH,
        )
        copy.start()
        pos_copies.append(copy)
    arrivals = [[] for _ in range(heads)]
    for a, (source, target, slot) in enumerate(pairs):
        copy = pltpu.make_async_copy(
            source.at[:, columns(mine)], target.at[slot], local_sem.at[a]
        )
        copy.start()
        arrivals[0].append(copy)
    for j in range(1, heads):
        other = lax.rem(mine + j, heads)
        for a, (source, target, slot) in enumerate(pairs):
            copy = pltpu.make_async_remote_copy(
                src_ref=source.at[:, columns(other)], dst_ref=target.at[slot],
                send_sem=in_send.at[a, j], recv_sem=in_recv.at[a, j],
                device_id={"seq": other * ratio + lane, "head": group}, device_id_type=MESH,
            )
            copy.start()
            arrivals[j].append(copy)

    mate_copies = []

    def forward(j):
        slot = lane * heads + lax.rem(mine + heads - j, heads)
        for a, buf in enumerate((k_buf, v_buf)):
            for m in range(1, ratio):
                copy = pltpu.make_async_remote_copy(
                    src_ref=buf.at[slot], dst_ref=buf.at[slot],
                    send_sem=mate_send.at[a, m, j], recv_sem=mate_recv.at[a, m, j],
                    device_id={"seq": mine * ratio + lax.rem(lane + m, ratio), "head": group},
                    device_id_type=MESH,
                )
                copy.start()
                mate_copies.append(copy)

    for j in range(heads):
        for a in range(2):
            arrivals[j][a].wait()
        forward(j)

    for copy in pos_copies:
        copy.wait()
    pos_buf[my_slot] = pos_ref[...]

    def spread(slot, carry):
        row = jnp.broadcast_to(pos_buf[slot][0:1, :], (HEAD_DIM, width))
        key_pos[slot] = row.T[:rows]
        return carry

    lax.fori_loop(0, members, spread, 0)
    for j in range(heads):
        for a in range(2, 4):
            arrivals[j][a].wait()
    for copy in mate_copies:
        copy.wait()

    per_block = q_buf.shape[0] if heads % 4 else 4
    blocks = heads // per_block
    block = per_block * rows
    part_rows = rows // groups

    dq_copies = []
    for b in range(blocks):
        sources = [
            lax.rem(mine + heads - (b * per_block + x), heads) for x in range(per_block)
        ]
        query = jnp.concatenate([q_buf[i] for i in sources], axis=0)
        grad = jnp.concatenate([g_buf[i] for i in sources], axis=0)
        for x, i in enumerate(sources):
            query_pos[x * rows:(x + 1) * rows, :] = key_pos[lane * heads + i]
        pos_row = query_pos[...].T[0:1, :]

        def scores_turn(slot, top):
            scores = lax.dot_general(k_buf[slot], query, NT, preferred_element_type=jnp.float32)
            held = jnp.concatenate([key_pos[slot]] * (block // HEAD_DIM), axis=1)
            scores = jnp.where(held <= pos_row, scores * scaling, -1e30)
            z_buf[slot] = scores
            return jnp.maximum(top, jnp.max(scores.reshape(rows // 8, 8, block), axis=0))

        top = lax.fori_loop(
            0, members, scores_turn, jnp.full((8, block), -1e30, jnp.float32)
        )
        top = jnp.max(top, axis=0, keepdims=True)

        def stats_turn(slot, carry):
            total, delta = carry
            unscaled = jnp.exp(z_buf[slot] - top)
            probs = lax.dot_general(v_buf[slot], grad, NT, preferred_element_type=jnp.float32)
            z_buf[slot] = unscaled
            p_buf[slot] = probs
            total = total + jnp.sum(unscaled.reshape(rows // 8, 8, block), axis=0)
            delta = delta + jnp.sum((unscaled * probs).reshape(rows // 8, 8, block), axis=0)
            return total, delta

        zero = jnp.zeros((8, block), jnp.float32)
        total, delta = lax.fori_loop(0, members, stats_turn, (zero, zero))
        inverse = 1.0 / jnp.sum(total, axis=0, keepdims=True)
        delta = jnp.sum(delta, axis=0, keepdims=True) * inverse

        dq_acc[...] = jnp.zeros_like(dq_acc)

        def terms(slot):
            weights = z_buf[slot] * inverse
            value_term = jnp.dot(
                weights.astype(jnp.bfloat16), grad, preferred_element_type=jnp.float32
            )
            grad_scores = (weights * ((p_buf[slot] - delta) * scaling)).astype(jnp.bfloat16)
            key_term = jnp.dot(grad_scores, query, preferred_element_type=jnp.float32)
            dq_acc[...] += lax.dot_general(
                k_buf[slot], grad_scores, TN, preferred_element_type=jnp.float32
            )
            if b > 0:
                key_term = key_term + dk_acc[slot]
                value_term = value_term + dv_acc[slot]
            return key_term, value_term

        if b < blocks - 1:

            def grads_turn(slot, carry):
                key_term, value_term = terms(slot)
                dk_acc[slot] = key_term
                dv_acc[slot] = value_term
                return carry

            lax.fori_loop(0, members, grads_turn, 0)
        else:
            def part_copy(m, i):
                other = lax.rem(lane + m, ratio)
                return pltpu.make_async_remote_copy(
                    src_ref=kv_stage.at[m - 1, i], dst_ref=kv_mates.at[m - 1, i],
                    send_sem=part_send.at[m, i], recv_sem=part_recv.at[m, i],
                    device_id={"seq": mine * ratio + other, "head": group}, device_id_type=MESH,
                )

            for m in range(1, ratio):

                def mate_turn(j, carry):
                    i = lax.rem(mine + 1 + j, heads)
                    slot = lax.rem(lane + m, ratio) * heads + i
                    key_term, value_term = terms(slot)
                    kv_stage[m - 1, i, 0] = key_term.astype(jnp.bfloat16)
                    kv_stage[m - 1, i, 1] = value_term.astype(jnp.bfloat16)
                    part_copy(m, i).start()
                    return carry

                lax.fori_loop(0, heads, mate_turn, 0)

            def back_copy(j):
                i = lax.rem(mine + 1 + j, heads)
                return pltpu.make_async_remote_copy(
                    src_ref=kv_final.at[i], dst_ref=kv_back.at[mine],
                    send_sem=back_send.at[j], recv_sem=back_recv.at[j],
                    device_id={"seq": i * ratio + lane, "head": group}, device_id_type=MESH,
                )

            def own_turn(j):
                i = lax.rem(mine + 1 + j, heads)
                key_term, value_term = terms(lane * heads + i)
                for m in range(1, ratio):
                    part_copy(m, i).wait()
                    key_term = key_term + kv_mates[m - 1, i, 0].astype(jnp.float32)
                    value_term = value_term + kv_mates[m - 1, i, 1].astype(jnp.float32)
                return i, key_term.astype(jnp.bfloat16), value_term.astype(jnp.bfloat16)

            def own_step(j, carry):
                i, key_term, value_term = own_turn(j)
                kv_final[i, 0] = key_term
                kv_final[i, 1] = value_term
                back_copy(j).start()
                return carry

            lax.fori_loop(0, heads - 1, own_step, 0)
            i, key_term, value_term = own_turn(heads - 1)
            kv_back[i, 0] = key_term
            kv_back[i, 1] = value_term

        grad_query = dq_acc[...].T
        for x, i in enumerate(sources):
            j = b * per_block + x
            for e in range(groups):
                other = lax.rem(group + e, groups)
                for r in range(groups):
                    if e == 0:
                        start = x * rows + r * part_rows
                        dq_stage[j, r] = grad_query[start:start + part_rows].astype(jnp.bfloat16)
            for e in range(groups):
                other = lax.rem(group + e, groups)
                if j == 0 and e == 0:
                    dq_back[group * heads + mine] = dq_stage[j, group]
                    continue
                copy = pltpu.make_async_remote_copy(
                    src_ref=dq_stage.at[j, other], dst_ref=dq_back.at[group * heads + mine],
                    send_sem=dq_send.at[j, e], recv_sem=dq_recv.at[j, e],
                    device_id={"seq": i * ratio + lane, "head": other}, device_id_type=MESH,
                )
                copy.start()
                dq_copies.append(copy)

    for j in range(heads - 1):
        back_copy(j).wait()
    for h in range(heads):
        dk_out[:, h * HEAD_DIM:(h + 1) * HEAD_DIM] = kv_back[h, 0]
        dv_out[:, h * HEAD_DIM:(h + 1) * HEAD_DIM] = kv_back[h, 1]
    for copy in dq_copies:
        copy.wait()
    for h in range(groups * heads):
        dq_out[:, h * HEAD_DIM:(h + 1) * HEAD_DIM] = dq_back[h]


def local(members, groups, query_rows, key_rows, value_rows, grad_output, positions):
    rows, wide = query_rows.shape
    heads = wide // HEAD_DIM
    ratio = members // heads
    width = -(-rows // HEAD_DIM) * HEAD_DIM
    per_block = heads if heads % 4 else 4
    block = per_block * rows
    position_rows = jnp.broadcast_to(
        jnp.pad(positions.astype(jnp.float32), (0, width - rows))[None], (8, width)
    )
    low, full = jnp.bfloat16, jnp.float32
    piece = (rows, HEAD_DIM)
    dma = pltpu.SemaphoreType.DMA
    scratch = [
        pltpu.VMEM((heads,) + piece, low),
        pltpu.VMEM((heads,) + piece, low),
        pltpu.VMEM((members,) + piece, low),
        pltpu.VMEM((members,) + piece, low),
        pltpu.VMEM((members, 8, width), full),
        pltpu.VMEM((members,) + piece, full),
        pltpu.VMEM((block, HEAD_DIM), full),
        pltpu.VMEM((members, rows, block), full),
        pltpu.VMEM((members, rows, block), full),
        pltpu.VMEM((members,) + piece, full),
        pltpu.VMEM((members,) + piece, full),
        pltpu.VMEM((HEAD_DIM, block), full),
        pltpu.VMEM((max(ratio - 1, 1), heads, 2) + piece, low),
        pltpu.VMEM((max(ratio - 1, 1), heads, 2) + piece, low),
        pltpu.VMEM((heads, 2) + piece, low),
        pltpu.VMEM((heads, 2) + piece, low),
        pltpu.VMEM((heads, groups, rows // groups, HEAD_DIM), low),
        pltpu.VMEM((groups * heads, rows // groups, HEAD_DIM), low),
        dma((4,)), dma((4, heads)), dma((4, heads)), dma((members,)), dma((members,)),
        dma((2, ratio, heads)), dma((2, ratio, heads)),
        dma((ratio, heads)), dma((ratio, heads)), dma((heads,)), dma((heads,)),
        dma((heads, groups)), dma((heads, groups)),
    ]
    vmem = pl.BlockSpec(memory_space=pltpu.VMEM)
    hbm = pl.BlockSpec(memory_space=pl.ANY)
    return pl.pallas_call(
        functools.partial(kernel, members, heads, groups, rows, width),
        out_shape=(
            jax.ShapeDtypeStruct((rows // groups, groups * wide), low),
            jax.ShapeDtypeStruct((rows, wide), low),
            jax.ShapeDtypeStruct((rows, wide), low),
        ),
        in_specs=[vmem, hbm, hbm, hbm, hbm],
        out_specs=(vmem, vmem, vmem),
        scratch_shapes=scratch,
        compiler_params=pltpu.CompilerParams(
            collective_id=0, has_side_effects=True, vmem_limit_bytes=60 * 1024 * 1024
        ),
    )(position_rows, query_rows, key_rows, value_rows, grad_output)


def solution(mesh):
    placed = (P("seq", "head"), P("seq", "head"), P("seq", "head"), P("seq", "head"), P("seq"))
    return jax.shard_map(
        functools.partial(local, mesh.shape["seq"], mesh.shape["head"]),
        mesh=mesh,
        in_specs=placed,
        out_specs=(P(("seq", "head"), None), P("seq", "head"), P("seq", "head")),
        check_vma=False,
    )
```

time: 538 us -> 106 us (0.20)
  waiting for transfers between devices: 284 us -> 0 us
  Pallas kernels: 0 us -> 99.8 us
  matrix products: 89.8 us -> 0 us
  blocking collectives: 74.9 us -> 0 us
  local copies, waits for them, and re-layouts: 53.1 us -> 4.31 us
  other arithmetic: 19.1 us -> 0.68 us
  between operations: 14.5 us -> 0.65 us
    reduce_scatter x2 -> x0, waiting for transfers between devices: 258 us -> none  [the longest x1 136 us: local(): lax.psum_scatter(key_full, 'seq', scatter_dimension=0, tiled=True)]
    pallas_call x0 -> x1, Pallas kernels: none -> 99.8 us  [local(): pl.pallas_call(functools.partial(kernel, members, heads, groups, rows, wi...]
    dot_general x82 -> x0, matrix products: 89.8 us -> none  [the longest x16 20.3 us: gradient_terms(): jnp.einsum('hqk,qhd->khd', grad_scores, query_heads, preferred_element_ty...]
    unnamed x1 -> x0, blocking collectives: 65.2 us -> none
    all_gather x2 -> x0, waiting for transfers between devices: 23.8 us -> none  [the longest x1 23.8 us: local(): lax.all_gather(value_rows, 'seq', axis=0, tiled=True)]
    while x16 -> x0, local copies, waits for them, and re-layouts: 18.7 us -> none
    all_gather x2 -> x0, local copies, waits for them, and re-layouts: 17.4 us -> none  [the longest x1 8.74 us: local(): lax.all_gather(key_rows, 'seq', axis=0, tiled=True)]
    reduce_sum x1 -> x0, other arithmetic: 12.6 us -> none  [stats_update(): denominator = jnp.sum(unscaled, axis=2)]
  transfers between devices with their start and end apart: 4 -> 0, of which waited for: 3 -> 0; matrix products, arithmetic and copies ran while one was open for 8% -> 0% of each run, Pallas kernels for 0% -> 0%
where the time goes in v1:
time: 106 us; the launch traced here: 105 us
  Pallas kernels  99.8 us (94%)
  local copies, waits for them, and re-layouts  4.31 us (4%)
    pallas_call x1, Pallas kernels, local(): pl.pallas_call(functools.partial(kernel, members, heads, groups, rows, wi...  99.8 us
    unnamed x7, local copies, waits for them, and re-layouts  3.7 us

profile of v1, /device:TPU:0, one launch (start us, length us, event | category | flops | bytes accessed | tf_op | source)
XLA Modules:
  0.0 105.5 jit_solution(13042844276326032350)
XLA Ops:
  0.6 0.7 convert_element_type.5
  1.3 0.6 broadcast_in_dim.2.pos_ref
  1.9 99.8 %shard_map.76 = (bf16[96,2048]{1,0:T(8,128)(2,1)}, bf16[192,1024]{1,0:T(8,128)(2,1)}, bf16[192,1024]{1,0:T(8,128)(2,1)}) custom-call(f32[8,256]{1,0:T(8,128)} %broadcast_in_dim.2.pos_ref, bf16[192,1024]{1,0:T(8,128)(2,1)} %q_hbm.1, bf16[192,1024]{1,0:T(8,128)(2,1)} %k_hbm.1, bf16[192,1024]{1,0:T(8,128)(2,1)} %v_hbm.1, bf16[192,1024]{1,0:T(8,128)(2,1)} %g_hbm.1), custom_call_target="tpu_custom_call" | custom-call | tf_op jit(solution)/shard_map/pallas_call | solution.py:312
  101.7 0.0 copy-start.1
  101.7 1.8 %copy.11 = bf16[96,2048]{1,0:T(8,128)(2,1)} copy(bf16[96,2048]{1,0:T(8,128)(2,1)} %get-tuple-element.6) | data formatting | bytes 786432
  103.6 0.0 copy-done.1
  103.6 0.0 copy-start
  103.6 0.7 copy.12
  104.3 0.4 copy-done
  104.7 0.7 copy.13
  (1 shorter events, 0.0 us)
Async XLA Ops:
  101.7 1.8 %copy-start.1 = (bf16[192,1024]{1,0:T(8,128)(2,1)S(1)}, bf16[192,1024]{1,0:T(8,128)(2,1)}, u32[]{:S(2)}) copy-start(bf16[192,1024]{1,0:T(8,128)(2,1)} %get-tuple-element.7) | copy-start | bytes 1179652
  103.6 1.1 %copy-start = (bf16[192,1024]{1,0:T(8,128)(2,1)S(1)}, bf16[192,1024]{1,0:T(8,128)(2,1)}, u32[]{:S(2)}) copy-start(bf16[192,1024]{1,0:T(8,128)(2,1)} %get-tuple-element.8) | copy-start | bytes 1179652

commit v2 on v1

v2 whole, which is shorter than its diff:
```python
import functools

import jax
import jax.numpy as jnp
from jax import lax
from jax.experimental import pallas as pl
from jax.experimental.pallas import tpu as pltpu
from jax.sharding import PartitionSpec as P

HEAD_DIM = 128
MESH = pl.DeviceIdType.MESH
NT = (((1,), (1,)), ((), ()))
TN = (((0,), (0,)), ((), ()))


def kernel(
    members, heads, groups, rows, width,
    pos_ref, q_hbm, k_hbm, v_hbm, g_hbm,
    dq_out, dk_out, dv_out,
    qg_buf, kv_buf, qg_stage, kv_stage, pos_buf, key_pos, tops,
    z_buf, p_buf, dq_acc, part_stage, part_mates, kv_final, kv_back, dq_stage, dq_back,
    qg_local, kv_local, qg_send, qg_recv, kv_send, kv_recv, pos_send, pos_recv,
    mate_send, mate_recv, part_send, part_recv, back_send, back_recv, dq_send, dq_recv,
):
    ratio = members // heads
    me = lax.axis_index("seq")
    group = lax.axis_index("head")
    mine = me // ratio
    lane = lax.rem(me, ratio)
    scaling = HEAD_DIM ** (-0.5)
    block = heads * rows
    part_rows = rows // groups
    my_slot = lane * heads + mine

    def columns(index):
        return pl.ds(pl.multiple_of(index * HEAD_DIM, HEAD_DIM), HEAD_DIM)

    def local_copies(arrays, stage, first, sems, j):
        other = lax.rem(mine + j, heads)
        return [
            pltpu.make_async_copy(
                array.at[:, columns(other)],
                first.at[a] if j == 0 else stage.at[j, a],
                sems.at[a, j],
            )
            for a, array in enumerate(arrays)
        ]

    qg_locals = [
        local_copies((q_hbm, g_hbm), qg_stage, qg_buf.at[mine], qg_local, j) for j in range(heads)
    ]
    kv_locals = [
        local_copies((k_hbm, v_hbm), kv_stage, kv_buf.at[my_slot], kv_local, j)
        for j in range(heads)
    ]
    for copies in qg_locals[1:] + kv_locals[1:] + qg_locals[:1] + kv_locals[:1]:
        for copy in copies:
            copy.start()

    barrier = pltpu.get_barrier_semaphore()
    for d in range(1, members):
        pl.semaphore_signal(
            barrier, inc=1,
            device_id={"seq": lax.rem(me + d, members), "head": group}, device_id_type=MESH,
        )
    for e in range(1, groups):
        for j in range(heads):
            pl.semaphore_signal(
                barrier, inc=1,
                device_id={
                    "seq": lax.rem(mine + j, heads) * ratio + lane,
                    "head": lax.rem(group + e, groups),
                },
                device_id_type=MESH,
            )
    pl.semaphore_wait(barrier, members - 1 + (groups - 1) * heads)

    def qg_copy(j):
        return pltpu.make_async_remote_copy(
            src_ref=qg_stage.at[j], dst_ref=qg_buf.at[mine],
            send_sem=qg_send.at[j], recv_sem=qg_recv.at[j],
            device_id={"seq": lax.rem(mine + j, heads) * ratio + lane, "head": group},
            device_id_type=MESH,
        )

    def kv_copy(j):
        return pltpu.make_async_remote_copy(
            src_ref=kv_stage.at[j], dst_ref=kv_buf.at[my_slot],
            send_sem=kv_send.at[j], recv_sem=kv_recv.at[j],
            device_id={"seq": lax.rem(mine + j, heads) * ratio + lane, "head": group},
            device_id_type=MESH,
        )

    def pos_copy(d):
        return pltpu.make_async_remote_copy(
            src_ref=pos_ref, dst_ref=pos_buf.at[my_slot],
            send_sem=pos_send.at[d], recv_sem=pos_recv.at[d],
            device_id={"seq": lax.rem(me + d, members), "head": group}, device_id_type=MESH,
        )

    for d in range(1, members):
        pos_copy(d).start()
    for j in range(1, heads):
        for copy in qg_locals[j]:
            copy.wait()
        qg_copy(j).start()
    for j in range(1, heads):
        for copy in kv_locals[j]:
            copy.wait()
        kv_copy(j).start()

    def mate_copy(m, j):
        slot = lane * heads + lax.rem(mine + heads - j, heads)
        return pltpu.make_async_remote_copy(
            src_ref=kv_buf.at[slot], dst_ref=kv_buf.at[slot],
            send_sem=mate_send.at[m, j], recv_sem=mate_recv.at[m, j],
            device_id={"seq": mine * ratio + lax.rem(lane + m, ratio), "head": group},
            device_id_type=MESH,
        )

    pos_buf[my_slot] = pos_ref[...]
    for d in range(1, members):
        pos_copy(d).wait()

    def spread(slot, carry):
        row = jnp.broadcast_to(pos_buf[slot][0:1, :], (HEAD_DIM, width))
        key_pos[slot] = row.T[:rows]
        return carry

    lax.fori_loop(0, members, spread, 0)
    held = key_pos[pl.ds(lane * heads, heads)].reshape(block, HEAD_DIM)
    pos_row = held.T[0:1, :]
    for copy in qg_locals[0] + kv_locals[0]:
        copy.wait()
    for j in range(1, heads):
        qg_copy(j).wait()

    def eights(values):
        return values.reshape(rows // 8, 8, block)

    def stats(slot, carry):
        top, total, delta = carry
        query = qg_buf[:, 0].reshape(block, HEAD_DIM)
        grad = qg_buf[:, 1].reshape(block, HEAD_DIM)
        scores = lax.dot_general(kv_buf[slot, 0], query, NT, preferred_element_type=jnp.float32)
        key_held = jnp.concatenate([key_pos[slot]] * (block // HEAD_DIM), axis=1)
        scores = jnp.where(key_held <= pos_row, scores * scaling, -1e30)
        here = jnp.max(jnp.max(eights(scores), axis=0), axis=0, keepdims=True)
        new_top = jnp.maximum(top, here)
        unscaled = jnp.exp(scores - new_top)
        probs = lax.dot_general(kv_buf[slot, 1], grad, NT, preferred_element_type=jnp.float32)
        z_buf[slot] = unscaled
        p_buf[slot] = probs
        tops[slot] = jnp.broadcast_to(new_top, (8, block))
        alpha = jnp.exp(top - new_top)
        total = total * alpha + jnp.sum(eights(unscaled), axis=0)
        delta = delta * alpha + jnp.sum(eights(unscaled * probs), axis=0)
        return new_top, total, delta

    def arrive_turn(j, carry):
        i = lax.rem(mine + heads - j, heads)

        @pl.when(j > 0)
        def _():
            kv_copy(j).wait()

        def start_turn(m, inner):
            mate_copy(m, j).start()
            return inner

        lax.fori_loop(1, ratio, start_turn, 0)
        carry = stats(lane * heads + i, carry)

        def mate_turn(m, inner):
            mate_copy(m, j).wait()
            return stats(lax.rem(lane + ratio - m, ratio) * heads + i, inner)

        return lax.fori_loop(1, ratio, mate_turn, carry)

    zero = jnp.zeros((8, block), jnp.float32)
    top, total, delta = lax.fori_loop(
        0, heads, arrive_turn, (jnp.full((1, block), -1e30, jnp.float32), zero, zero)
    )
    inverse = 1.0 / jnp.sum(total, axis=0, keepdims=True)
    delta = jnp.sum(delta, axis=0, keepdims=True) * inverse
    dq_acc[...] = jnp.zeros_like(dq_acc)

    def terms(slot):
        query = qg_buf[:, 0].reshape(block, HEAD_DIM)
        grad = qg_buf[:, 1].reshape(block, HEAD_DIM)
        weights = z_buf[slot] * (jnp.exp(tops[slot][0:1] - top) * inverse)
        value_term = jnp.dot(
            weights.astype(jnp.bfloat16), grad, preferred_element_type=jnp.float32
        )
        grad_scores = (weights * ((p_buf[slot] - delta) * scaling)).astype(jnp.bfloat16)
        key_term = jnp.dot(grad_scores, query, preferred_element_type=jnp.float32)
        dq_acc[...] += lax.dot_general(
            kv_buf[slot, 0], grad_scores, TN, preferred_element_type=jnp.float32
        )
        return key_term, value_term

    def part_copy(m, i):
        return pltpu.make_async_remote_copy(
            src_ref=part_stage.at[m - 1, i], dst_ref=part_mates.at[m - 1, i],
            send_sem=part_send.at[m, i], recv_sem=part_recv.at[m, i],
            device_id={"seq": mine * ratio + lax.rem(lane + m, ratio), "head": group},
            device_id_type=MESH,
        )

    def mate_parts(m, carry):
        def mate_part(j, inner):
            i = lax.rem(mine + 1 + j, heads)
            key_term, value_term = terms(lax.rem(lane + m, ratio) * heads + i)
            part_stage[m - 1, i, 0] = key_term.astype(jnp.bfloat16)
            part_stage[m - 1, i, 1] = value_term.astype(jnp.bfloat16)
            part_copy(m, i).start()
            return inner

        return lax.fori_loop(0, heads, mate_part, carry)

    lax.fori_loop(1, ratio, mate_parts, 0)

    def back_copy(j):
        i = lax.rem(mine + 1 + j, heads)
        return pltpu.make_async_remote_copy(
            src_ref=kv_final.at[i], dst_ref=kv_back.at[mine],
            send_sem=back_send.at[j], recv_sem=back_recv.at[j],
            device_id={"seq": i * ratio + lane, "head": group}, device_id_type=MESH,
        )

    def own_step(j, carry):
        i = lax.rem(mine + 1 + j, heads)
        key_term, value_term = terms(lane * heads + i)
        for m in range(1, ratio):
            part_copy(m, i).wait()
            key_term = key_term + part_mates[m - 1, i, 0].astype(jnp.float32)
            value_term = value_term + part_mates[m - 1, i, 1].astype(jnp.float32)
        kv_final[i, 0] = key_term.astype(jnp.bfloat16)
        kv_final[i, 1] = value_term.astype(jnp.bfloat16)

        @pl.when(j < heads - 1)
        def _():
            back_copy(j).start()

        return carry

    lax.fori_loop(0, heads, own_step, 0)
    kv_back[mine] = kv_final[mine]

    grad_query = dq_acc[...].T.astype(jnp.bfloat16)
    dq_stage[...] = grad_query.reshape(heads, groups, part_rows, HEAD_DIM)

    def dq_copy(j, e):
        i = lax.rem(mine + 1 + j, heads)
        other = lax.rem(group + e, groups)
        return pltpu.make_async_remote_copy(
            src_ref=dq_stage.at[i, other], dst_ref=dq_back.at[group * heads + mine],
            send_sem=dq_send.at[j, e], recv_sem=dq_recv.at[j, e],
            device_id={"seq": i * ratio + lane, "head": other}, device_id_type=MESH,
        )

    remote = [(j, e) for j in range(heads) for e in range(groups) if (j, e) != (heads - 1, 0)]
    for j, e in remote:
        dq_copy(j, e).start()
    dq_back[group * heads + mine] = dq_stage[mine, group]

    for j in range(heads - 1):
        back_copy(j).wait()
    for h in range(heads):
        dk_out[:, h * HEAD_DIM:(h + 1) * HEAD_DIM] = kv_back[h, 0]
        dv_out[:, h * HEAD_DIM:(h + 1) * HEAD_DIM] = kv_back[h, 1]
    for j, e in remote:
        dq_copy(j, e).wait()
    for h in range(groups * heads):
        dq_out[:, h * HEAD_DIM:(h + 1) * HEAD_DIM] = dq_back[h]


def local(members, groups, query_rows, key_rows, value_rows, grad_output, positions):
    rows, wide = query_rows.shape
    heads = wide // HEAD_DIM
    ratio = members // heads
    width = -(-rows // HEAD_DIM) * HEAD_DIM
    block = heads * rows
    position_rows = jnp.broadcast_to(
        jnp.pad(positions.astype(jnp.float32), (0, width - rows))[None], (8, width)
    )
    low, full = jnp.bfloat16, jnp.float32
    piece = (rows, HEAD_DIM)
    dma = pltpu.SemaphoreType.DMA
    mates = max(ratio - 1, 1)
    scratch = [
        pltpu.VMEM((heads, 2) + piece, low),
        pltpu.VMEM((members, 2) + piece, low),
        pltpu.VMEM((heads, 2) + piece, low),
        pltpu.VMEM((heads, 2) + piece, low),
        pltpu.VMEM((members, 8, width), full),
        pltpu.VMEM((members,) + piece, full),
        pltpu.VMEM((members, 8, block), full),
        pltpu.VMEM((members, rows, block), full),
        pltpu.VMEM((members, rows, block), full),
        pltpu.VMEM((HEAD_DIM, block), full),
        pltpu.VMEM((mates, heads, 2) + piece, low),
        pltpu.VMEM((mates, heads, 2) + piece, low),
        pltpu.VMEM((heads, 2) + piece, low),
        pltpu.VMEM((heads, 2) + piece, low),
        pltpu.VMEM((heads, groups, rows // groups, HEAD_DIM), low),
        pltpu.VMEM((groups * heads, rows // groups, HEAD_DIM), low),
        dma((2, heads)), dma((2, heads)), dma((heads,)), dma((heads,)), dma((heads,)),
        dma((heads,)), dma((members,)), dma((members,)),
        dma((ratio, heads)), dma((ratio, heads)),
        dma((ratio, heads)), dma((ratio, heads)), dma((heads,)), dma((heads,)),
        dma((heads, groups)), dma((heads, groups)),
    ]
    vmem = pl.BlockSpec(memory_space=pltpu.VMEM)
    hbm = pl.BlockSpec(memory_space=pl.ANY)
    return pl.pallas_call(
        functools.partial(kernel, members, heads, groups, rows, width),
        out_shape=(
            jax.ShapeDtypeStruct((rows // groups, groups * wide), low),
            jax.ShapeDtypeStruct((rows, wide), low),
            jax.ShapeDtypeStruct((rows, wide), low),
        ),
        in_specs=[vmem, hbm, hbm, hbm, hbm],
        out_specs=(vmem, vmem, vmem),
        scratch_shapes=scratch,
        compiler_params=pltpu.CompilerParams(
            collective_id=0, has_side_effects=True, vmem_limit_bytes=63 * 1024 * 1024
        ),
    )(position_rows, query_rows, key_rows, value_rows, grad_output)


def solution(mesh):
    placed = (P("seq", "head"), P("seq", "head"), P("seq", "head"), P("seq", "head"), P("seq"))
    return jax.shard_map(
        functools.partial(local, mesh.shape["seq"], mesh.shape["head"]),
        mesh=mesh,
        in_specs=placed,
        out_specs=(P(("seq", "head"), None), P("seq", "head"), P("seq", "head")),
        check_vma=False,
    )
```

time: 106 us -> 94.6 us (0.89)
  Pallas kernels: 99.8 us -> 87.8 us
    pallas_call x1, Pallas kernels: 99.8 us -> 87.8 us  [local(): pl.pallas_call(functools.partial(kernel, members, heads, groups, rows, wi...]
where the time goes in v2:
time: 94.6 us; the launch traced here: 93.4 us
  Pallas kernels  87.8 us (93%)
  local copies, waits for them, and re-layouts  4.31 us (5%)
    pallas_call x1, Pallas kernels, local(): pl.pallas_call(functools.partial(kernel, members, heads, groups, rows, wi...  87.8 us
    unnamed x7, local copies, waits for them, and re-layouts  3.7 us

profile of v2, /device:TPU:0, one launch (start us, length us, event | category | flops | bytes accessed | tf_op | source)
XLA Modules:
  0.0 93.4 jit_solution(7769873405836215871)
XLA Ops:
  0.6 0.7 convert_element_type.5
  1.3 0.6 broadcast_in_dim.2.pos_ref
  1.9 87.8 %shard_map.76 = (bf16[96,2048]{1,0:T(8,128)(2,1)}, bf16[192,1024]{1,0:T(8,128)(2,1)}, bf16[192,1024]{1,0:T(8,128)(2,1)}) custom-call(f32[8,256]{1,0:T(8,128)} %broadcast_in_dim.2.pos_ref, bf16[192,1024]{1,0:T(8,128)(2,1)} %q_hbm.1, bf16[192,1024]{1,0:T(8,128)(2,1)} %k_hbm.1, bf16[192,1024]{1,0:T(8,128)(2,1)} %v_hbm.1, bf16[192,1024]{1,0:T(8,128)(2,1)} %g_hbm.1), custom_call_target="tpu_custom_call" | custom-call | tf_op jit(solution)/shard_map/pallas_call | solution.py:316
  89.7 0.0 copy-start.1
  89.7 1.8 %copy.11 = bf16[96,2048]{1,0:T(8,128)(2,1)} copy(bf16[96,2048]{1,0:T(8,128)(2,1)} %get-tuple-element.6) | data formatting | bytes 786432
  91.5 0.0 copy-done.1
  91.6 0.0 copy-start
  91.6 0.7 copy.12
  92.3 0.4 copy-done
  92.7 0.7 copy.13
  (1 shorter events, 0.0 us)
Async XLA Ops:
  89.7 1.8 %copy-start.1 = (bf16[192,1024]{1,0:T(8,128)(2,1)S(1)}, bf16[192,1024]{1,0:T(8,128)(2,1)}, u32[]{:S(2)}) copy-start(bf16[192,1024]{1,0:T(8,128)(2,1)} %get-tuple-element.7) | copy-start | bytes 1179652
  91.6 1.1 %copy-start = (bf16[192,1024]{1,0:T(8,128)(2,1)S(1)}, bf16[192,1024]{1,0:T(8,128)(2,1)}, u32[]{:S(2)}) copy-start(bf16[192,1024]{1,0:T(8,128)(2,1)} %get-tuple-element.8) | copy-start | bytes 1179652

commit v3 on v2

--- a/solution.py
+++ b/solution.py
@@ -157,29 +157,32 @@
         delta = delta * alpha + jnp.sum(eights(unscaled * probs), axis=0)
         return new_top, total, delta
 
-    def arrive_turn(j, carry):
+    def arrive_turn(step, carry):
+        j = step // ratio
+        m = lax.rem(step, ratio)
         i = lax.rem(mine + heads - j, heads)
 
-        @pl.when(j > 0)
+        @pl.when((m == 0) & (j > 0))
         def _():
             kv_copy(j).wait()
 
-        def start_turn(m, inner):
-            mate_copy(m, j).start()
-            return inner
-
-        lax.fori_loop(1, ratio, start_turn, 0)
-        carry = stats(lane * heads + i, carry)
-
-        def mate_turn(m, inner):
+        @pl.when(m == 0)
+        def _():
+            def start_turn(other, inner):
+                mate_copy(other, j).start()
+                return inner
+
+            lax.fori_loop(1, ratio, start_turn, 0)
+
+        @pl.when(m > 0)
+        def _():
             mate_copy(m, j).wait()
-            return stats(lax.rem(lane + ratio - m, ratio) * heads + i, inner)
-
-        return lax.fori_loop(1, ratio, mate_turn, carry)
+
+        return stats(lax.rem(lane + ratio - m, ratio) * heads + i, carry)
 
     zero = jnp.zeros((8, block), jnp.float32)
     top, total, delta = lax.fori_loop(
-        0, heads, arrive_turn, (jnp.full((1, block), -1e30, jnp.float32), zero, zero)
+        0, members, arrive_turn, (jnp.full((1, block), -1e30, jnp.float32), zero, zero)
     )
     inverse = 1.0 / jnp.sum(total, axis=0, keepdims=True)
     delta = jnp.sum(delta, axis=0, keepdims=True) * inverse
@@ -207,19 +210,6 @@
             device_id_type=MESH,
         )
 
-    def mate_parts(m, carry):
-        def mate_part(j, inner):
-            i = lax.rem(mine + 1 + j, heads)
-            key_term, value_term = terms(lax.rem(lane + m, ratio) * heads + i)
-            part_stage[m - 1, i, 0] = key_term.astype(jnp.bfloat16)
-            part_stage[m - 1, i, 1] = value_term.astype(jnp.bfloat16)
-            part_copy(m, i).start()
-            return inner
-
-        return lax.fori_loop(0, heads, mate_part, carry)
-
-    lax.fori_loop(1, ratio, mate_parts, 0)
-
     def back_copy(j):
         i = lax.rem(mine + 1 + j, heads)
         return pltpu.make_async_remote_copy(
@@ -228,7 +218,14 @@
             device_id={"seq": i * ratio + lane, "head": group}, device_id_type=MESH,
         )
 
-    def own_step(j, carry):
+    def mate_part(m, j):
+        i = lax.rem(mine + 1 + j, heads)
+        key_term, value_term = terms(lax.rem(lane + m, ratio) * heads + i)
+        part_stage[m - 1, i, 0] = key_term.astype(jnp.bfloat16)
+        part_stage[m - 1, i, 1] = value_term.astype(jnp.bfloat16)
+        part_copy(m, i).start()
+
+    def own_part(j):
         i = lax.rem(mine + 1 + j, heads)
         key_term, value_term = terms(lane * heads + i)
         for m in range(1, ratio):
@@ -242,9 +239,22 @@
         def _():
             back_copy(j).start()
 
+    def grads_turn(j, carry):
+        @pl.when(j < heads)
+        def _():
+            def mate_turn(m, inner):
+                mate_part(m, j)
+                return inner
+
+            lax.fori_loop(1, ratio, mate_turn, 0)
+
+        @pl.when(j > 0)
+        def _():
+            own_part(j - 1)
+
         return carry
 
-    lax.fori_loop(0, heads, own_step, 0)
+    lax.fori_loop(0, heads + 1, grads_turn, 0)
     kv_back[mine] = kv_final[mine]
 
     grad_query = dq_acc[...].T.astype(jnp.bfloat16)

time: 94.6 us -> 91.8 us (0.970)
  Pallas kernels: 87.8 us -> 85 us
    pallas_call x1, Pallas kernels: 87.8 us -> 85 us  [local(): pl.pallas_call(functools.partial(kernel, members, heads, groups, rows, wi...]
where the time goes in v3:
time: 91.8 us; the launch traced here: 90.6 us
  Pallas kernels  85 us (93%)
  local copies, waits for them, and re-layouts  4.31 us (5%)
    pallas_call x1, Pallas kernels, local(): pl.pallas_call(functools.partial(kernel, members, heads, groups, rows, wi...  85 us
    unnamed x7, local copies, waits for them, and re-layouts  3.7 us

profile of v3, /device:TPU:0, one launch (start us, length us, event | category | flops | bytes accessed | tf_op | source)
XLA Modules:
  0.0 90.6 jit_solution(7067225824193640414)
XLA Ops:
  0.6 0.7 convert_element_type.5
  1.3 0.6 broadcast_in_dim.2.pos_ref
  1.9 85.0 %shard_map.76 = (bf16[96,2048]{1,0:T(8,128)(2,1)}, bf16[192,1024]{1,0:T(8,128)(2,1)}, bf16[192,1024]{1,0:T(8,128)(2,1)}) custom-call(f32[8,256]{1,0:T(8,128)} %broadcast_in_dim.2.pos_ref, bf16[192,1024]{1,0:T(8,128)(2,1)} %q_hbm.1, bf16[192,1024]{1,0:T(8,128)(2,1)} %k_hbm.1, bf16[192,1024]{1,0:T(8,128)(2,1)} %v_hbm.1, bf16[192,1024]{1,0:T(8,128)(2,1)} %g_hbm.1), custom_call_target="tpu_custom_call" | custom-call | tf_op jit(solution)/shard_map/pallas_call | solution.py:326
  86.9 0.0 copy-start.1
  86.9 1.8 %copy.11 = bf16[96,2048]{1,0:T(8,128)(2,1)} copy(bf16[96,2048]{1,0:T(8,128)(2,1)} %get-tuple-element.6) | data formatting | bytes 786432
  88.8 0.0 copy-done.1
  88.8 0.0 copy-start
  88.8 0.7 copy.12
  89.5 0.4 copy-done
  89.9 0.7 copy.13
  (1 shorter events, 0.0 us)
Async XLA Ops:
  86.9 1.8 %copy-start.1 = (bf16[192,1024]{1,0:T(8,128)(2,1)S(1)}, bf16[192,1024]{1,0:T(8,128)(2,1)}, u32[]{:S(2)}) copy-start(bf16[192,1024]{1,0:T(8,128)(2,1)} %get-tuple-element.7) | copy-start | bytes 1179652
  88.8 1.1 %copy-start = (bf16[192,1024]{1,0:T(8,128)(2,1)S(1)}, bf16[192,1024]{1,0:T(8,128)(2,1)}, u32[]{:S(2)}) copy-start(bf16[192,1024]{1,0:T(8,128)(2,1)} %get-tuple-element.8) | copy-start | bytes 1179652
